TPU v7x, 32 devices: a whole 2x2x4 slice. The times are simulated.
32 devices in a mesh: rows: 4 (over y, x), batch: 8 (over z, core).
Axes of the slice: x: 2, y: 2, z: 4, core: 2. Of those that a mesh axis runs over, the one named last changes fastest.
Arguments:
- control: bfloat16 [8, 24, 96, 320], P('batch', 'rows'), may hold values from -60 to 60, as said below
- unet_skips: bfloat16 [2, 8, 24, 96, 320], P(None, 'batch', 'rows'), may hold values from -6 to 6
- norm_gains: float32 [2, 2, 320], replicated, may hold values from 0.25 to 1.75
- norm_shifts: float32 [2, 2, 320], replicated, may hold values from -3 to 3
- conv_weights: bfloat16 [2, 2, 3, 960, 320], P(None, None, None, None, 'batch'), may hold values from -0.109375 to 0.109375
- zero_weights: bfloat16 [2, 1, 320, 320], P(None, None, None, 'batch'), may hold values from -0.3125 to 0.3125
Outputs:
- controls: bfloat16 [2, 8, 24, 96, 320], P(None, 'batch', 'rows')
Inputs may be any that keep to these rules, and one draw needn't show every extreme that they name: `control`: Real-valued latent features.
All inputs are finite; a program needn't handle non-finite values.
Results may differ from a plain program's by a relative error of at most 0.01.
Values may be sent and summed in bfloat16 or wider, within the bound.
A program may use at most 64 MiB of HBM per device.

v0:
```python
import functools

import jax
import jax.numpy as jnp
import numpy as np
from jax import lax
from jax.experimental import pallas as pl
from jax.experimental.pallas import tpu as pltpu
from jax.sharding import PartitionSpec as P

GROUPS = 32
EPSILON = 1e-05
MESH = pl.DeviceIdType.MESH


def transposed(conv_weights, zero_weights):
    blocks, convs, taps, depth, outs = conv_weights.shape
    conv = jnp.transpose(conv_weights, (0, 1, 2, 4, 3)).reshape(blocks * convs, taps * outs, depth)
    return conv, jnp.transpose(zero_weights[:, 0], (0, 2, 1))


def kernel(dims, x_ref, skip_ref, gain_ref, shift_ref, group_ref, w_ref, zw_ref, out_ref,
           slabs, wfull, zfull, stk, halo, fields, stat_out, stat_in,
           z_send, z_recv, a_send, a_recv, b_send, b_recv, d_send, d_recv,
           h_send, h_recv, t_send, t_recv):
    rows_n, batch_n, height, across, channels, outs, taps, members = dims
    convs, _, depth = w_ref.shape
    lanes = slabs.shape[3]
    piece = lanes - depth
    zn = batch_n // 2
    r = lax.axis_index("rows")
    b = lax.axis_index("batch")
    z, c = b // 2, b % 2
    bit0, bit1 = r % 2, (r // 2) % 2
    px, py = r + 1 - 2 * bit0, r + 2 - 4 * bit1
    p1 = (1 - c) * px + c * py
    p2 = (1 - c) * py + c * px
    q = (1 - c) * (2 * bit1 + bit0) + c * (2 * bit0 + bit1)
    mate = b + 1 - 2 * c
    quarter, half = lanes // 4, lanes // 2
    every = slice(None)
    mine = pl.ds(pl.multiple_of(q * quarter, quarter), quarter)
    peer = pl.ds(pl.multiple_of((q + 1 - 2 * (q % 2)) * quarter, quarter), quarter)
    my_half = pl.ds(pl.multiple_of((q // 2) * half, half), half)
    other_half = pl.ds(pl.multiple_of((1 - q // 2) * half, half), half)
    order = sorted(range(1, zn), key=lambda j: min(j, zn - j))

    def remote(src, dst, send, recv, row, batch):
        return pltpu.make_async_remote_copy(
            src_ref=src, dst_ref=dst, send_sem=send, recv_sem=recv,
            device_id={"rows": row, "batch": batch}, device_id_type=MESH)

    barrier = pltpu.get_barrier_semaphore()
    for j in range(1, zn):
        pl.semaphore_signal(barrier, inc=1, device_id_type=MESH,
                            device_id={"rows": r, "batch": ((z + j) % zn) * 2 + c})
    for j in range(1, rows_n):
        pl.semaphore_signal(barrier, inc=1, device_id_type=MESH,
                            device_id={"rows": (r + j) % rows_n, "batch": b})
    pl.semaphore_signal(barrier, inc=1, device_id_type=MESH, device_id={"rows": r, "batch": mate})

    pieces = -(-channels // piece)
    per_block = convs // zw_ref.shape[0]
    for k in range(convs):
        slabs[k, b, :, :depth] = w_ref[k]
        block = k // per_block
        for tap in range(taps):
            p = (k % per_block) * taps + tap
            if p < pieces:
                wide = min(piece, channels - p * piece)
                slabs[k, b, tap * outs:(tap + 1) * outs, depth:depth + wide] = (
                    zw_ref[block, :, p * piece:p * piece + wide])
    pl.semaphore_wait(barrier, zn + rows_n - 1)

    sent = []

    def start(copy):
        copy.start()
        sent.append(copy)

    def source(j):
        return ((z + zn - j) % zn) * 2 + c

    def z_start(k):
        here = slabs.at[k, b, every, mine]
        for j in order:
            start(remote(here, here, z_send.at[k, j], z_recv.at[k, j],
                         r, ((z + j) % zn) * 2 + c))

    def a_step(k):
        for j in order:
            s = source(j)
            here = slabs.at[k, s, every, mine]
            remote(here, here, z_send.at[k, j], z_recv.at[k, j], p1, b).wait_recv()
            start(remote(here, here, a_send.at[k, j], a_recv.at[k, j], p1, b))

    def b_step(k):
        for j in order:
            s = source(j)
            got = slabs.at[k, s, every, peer]
            remote(got, got, a_send.at[k, j], a_recv.at[k, j], p1, b).wait_recv()
            here = slabs.at[k, s, every, my_half]
            start(remote(here, here, b_send.at[k, j], b_recv.at[k, j], p2, b))

    def d_step(k):
        for j in order:
            s = source(j)
            got = slabs.at[k, s, every, other_half]
            remote(got, got, b_send.at[k, j], b_recv.at[k, j], p2, b).wait_recv()
            here = slabs.at[k, s]
            start(remote(here, here, d_send.at[k, j], d_recv.at[k, j], r, mate))

    def d_wait(k):
        for j in [0] + order:
            s = ((z + zn - j) % zn) * 2 + (1 - c)
            here = slabs.at[k, s]
            remote(here, here, d_send.at[k, j], d_recv.at[k, j], r, mate).wait_recv()

    def assemble(k):
        for d in range(batch_n):
            for tap in range(taps):
                wfull[tap, d * outs:(d + 1) * outs, :] = (
                    slabs[k, d, tap * outs:(tap + 1) * outs, :depth])

    def assemble_zero(block):
        for d in range(batch_n):
            parts = []
            for p in range(pieces):
                wide = min(piece, channels - p * piece)
                tap = p % taps
                parts.append(slabs[block * per_block + p // taps, d,
                                   tap * outs:(tap + 1) * outs, depth:depth + wide])
            zfull[d * outs:(d + 1) * outs, :] = jnp.concatenate(parts, axis=1)

    def times(a, w):
        return lax.dot_general(a, w, (((1,), (1,)), ((), ())), preferred_element_type=jnp.float32)

    def halo_start(s, ref):
        cells = height * across

        def down():
            return remote(ref.at[pl.ds(cells - across, across)], halo.at[s, 0],
                          h_send.at[s, 0], h_recv.at[s, 0], (r + 1) % rows_n, b)

        def up():
            return remote(ref.at[pl.ds(0, across)], halo.at[s, 1],
                          h_send.at[s, 1], h_recv.at[s, 1], (r + rows_n - 1) % rows_n, b)

        @pl.when(r < rows_n - 1)
        def _():
            down().start()

        @pl.when(r > 0)
        def _():
            up().start()

        return down, up

    def stat_start(s, total, square):
        stat_out[s] = jnp.concatenate([total, square, jnp.zeros((6, channels), jnp.float32)], axis=0)
        for j in range(1, rows_n):
            start(remote(stat_out.at[s], stat_in.at[s, j], t_send.at[s, j], t_recv.at[s, j],
                         (r + j) % rows_n, b))

    col = lax.broadcasted_iota(jnp.int32, (across, channels), 0)

    def normalize(s, ref):
        total = stat_out[s]
        for j in range(1, rows_n):
            here = stat_in.at[s, j]
            remote(here, here, t_send.at[s, j], t_recv.at[s, j], r, mate).wait_recv()
            total = total + stat_in[s, j]
        grouped = jnp.dot(total, group_ref[...], precision=lax.Precision.HIGHEST,
                          preferred_element_type=jnp.float32) * (1.0 / members)
        mean = grouped[0:1]
        spread = jnp.maximum(grouped[1:2] - mean * mean, 0.0)
        scale = lax.rsqrt(spread + EPSILON) * gain_ref[s:s + 1, :]
        bias = shift_ref[s:s + 1, :] - mean * scale

        def put(at, v, valid):
            y = v.astype(jnp.float32) * scale + bias
            a = y / (1.0 + jnp.exp(-y))
            if valid is not None:
                a = jnp.where(valid, a, 0.0)
            left = jnp.where(col == 0, 0.0, pltpu.roll(a, 1, 0))
            right = jnp.where(col == across - 1, 0.0, pltpu.roll(a, across - 1, 0))
            stk[pl.ds(at, across), :] = jnp.concatenate(
                [left.astype(jnp.bfloat16), a.astype(jnp.bfloat16), right.astype(jnp.bfloat16)], axis=1)

        def body(i, carry):
            at = pl.multiple_of(i * across, across)
            put(pl.multiple_of(at + across, across), ref[pl.ds(at, across), :], None)
            return carry
        lax.fori_loop(0, height, body, 0)
        return put

    def edges(s, put, ends):
        down, up = ends

        @pl.when(r > 0)
        def _():
            down().wait_recv()

        @pl.when(r < rows_n - 1)
        def _():
            up().wait_recv()

        put(0, halo[s, 0], r > 0)
        put((height + 1) * across, halo[s, 1], r < rows_n - 1)

    def inner():
        cells = (height - 2) * across
        total = None
        for tap in range(taps):
            at = (tap + 1) * across
            part = times(stk[at:at + cells, :], wfull[tap])
            total = part if total is None else total + part
        return total

    def outer():
        total = None
        for tap in range(taps):
            low, high = tap * across, (height - 1 + tap) * across
            both = jnp.concatenate([stk[low:low + across, :], stk[high:high + across, :]], axis=0)
            part = times(both, wfull[tap])
            total = part if total is None else total + part
        return total

    def convolve(s, put, ends, source):
        cells = height * across

        def keep(at, value):
            size = value.shape[0]
            if source is not None:
                value = source[at:at + size, :].astype(jnp.float32) + value
            value = value.astype(jnp.bfloat16)
            fields[s, at:at + size, :] = value
            kept = value.astype(jnp.float32)
            return (jnp.sum(kept, axis=0, keepdims=True),
                    jnp.sum(kept * kept, axis=0, keepdims=True))

        middle = keep(across, inner())
        edges(s, put, ends)
        border = outer()
        top = keep(0, border[:across])
        bottom = keep(cells - across, border[across:])
        return middle[0] + top[0] + bottom[0], middle[1] + top[1] + bottom[1]

    def zero_conv(s):
        block = s // per_block
        assemble_zero(block)
        zeroed = times(fields[s], zfull[...])
        out_ref[block] = (skip_ref[block].astype(jnp.float32) + zeroed).astype(jnp.bfloat16)

    ends = [halo_start(0, x_ref)]
    for k in range(convs):
        z_start(k)
        here = slabs.at[k, b]
        start(remote(here, here, d_send.at[k, 0], d_recv.at[k, 0], r, mate))
        if k == 0:
            first = x_ref[...].astype(jnp.float32)
            stat_start(0, jnp.sum(first, axis=0, keepdims=True),
                       jnp.sum(first * first, axis=0, keepdims=True))
    put = normalize(0, x_ref)
    a_step(0)
    b_step(0)
    a_step(1)
    d_step(0)
    b_step(1)
    source_ref = x_ref
    for s in range(convs):
        d_wait(s)
        assemble(s)
        if s + 2 < convs:
            a_step(s + 2)
        if s > 0:
            put = normalize(s, fields.at[s - 1])
        last = s % per_block == per_block - 1
        sums = convolve(s, put, ends[s], source_ref if last else None)
        if last:
            source_ref = fields.at[s]
        if s < convs - 1:
            stat_start(s + 1, *sums)
            ends.append(halo_start(s + 1, fields.at[s]))
        if s + 1 < convs:
            d_step(s + 1)
        if s + 2 < convs:
            b_step(s + 2)
        if last:
            zero_conv(s)
    for copy in sent:
        copy.wait_send()
    for down, up in ends:
        @pl.when(r < rows_n - 1)
        def _():
            down().wait_send()

        @pl.when(r > 0)
        def _():
            up().wait_send()


def on_device(rows_n, batch_n, control, unet_skips, norm_gains, norm_shifts, conv_weights, zero_weights):
    blocks, convs, taps, depth, outs = conv_weights.shape
    samples, height, across, channels = control.shape
    lanes = (depth // 512 + 1) * 512
    stages = blocks * convs
    cells = height * across
    per = channels // GROUPS
    member = np.arange(channels) // per
    group = jnp.asarray((member[:, None] == member[None, :]).astype(np.float32))
    conv, zero = transposed(conv_weights, zero_weights)
    members = cells * rows_n * per
    dims = (rows_n, batch_n, height, across, channels, outs, taps, members)
    zn = batch_n // 2
    dma = pltpu.SemaphoreType.DMA
    vmem = pl.BlockSpec(memory_space=pltpu.VMEM)
    out = pl.pallas_call(
        functools.partial(kernel, dims),
        out_shape=jax.ShapeDtypeStruct((blocks, cells, channels), jnp.bfloat16),
        in_specs=[vmem] * 7,
        out_specs=vmem,
        scratch_shapes=[
            pltpu.VMEM((stages, batch_n, taps * outs, lanes), jnp.bfloat16),
            pltpu.VMEM((taps, channels, depth), jnp.bfloat16),
            pltpu.VMEM((channels, channels), jnp.bfloat16),
            pltpu.VMEM(((height + taps - 1) * across, depth), jnp.bfloat16),
            pltpu.VMEM((stages, 2, across, channels), jnp.bfloat16),
            pltpu.VMEM((stages, cells, channels), jnp.bfloat16),
            pltpu.VMEM((stages, 8, channels), jnp.float32),
            pltpu.VMEM((stages, rows_n, 8, channels), jnp.float32),
            dma((stages, zn)), dma((stages, zn)),
            dma((stages, zn)), dma((stages, zn)),
            dma((stages, zn)), dma((stages, zn)),
            dma((stages, zn)), dma((stages, zn)),
            dma((stages, 2)), dma((stages, 2)),
            dma((stages, rows_n)), dma((stages, rows_n)),
        ],
        compiler_params=pltpu.CompilerParams(
            collective_id=0, has_side_effects=True, vmem_limit_bytes=50 * 1024 * 1024),
    )(
        control.reshape(cells, channels),
        unet_skips.reshape(blocks, cells, channels),
        norm_gains.reshape(stages, channels),
        norm_shifts.reshape(stages, channels),
        group,
        conv,
        zero,
    )
    return out.reshape(blocks, samples, height, across, channels)


def solution(mesh):
    placed = (
        P("batch", "rows", None, None),
        P(None, "batch", "rows", None, None),
        P(),
        P(),
        P(None, None, None, None, "batch"),
        P(None, None, None, "batch"),
    )
    return jax.shard_map(
        functools.partial(on_device, mesh.shape["rows"], mesh.shape["batch"]),
        mesh=mesh,
        in_specs=placed,
        out_specs=P(None, "batch", "rows", None, None),
        check_vma=False,
    )
```

profile of v0, /device:TPU:0, one launch (start us, length us, event | category | flops | bytes accessed | tf_op | source)
XLA Modules:
  0.0 64.1 jit_solution(8235109225513479079)
XLA Ops:
  0.0 0.0 copy-start.5
  0.0 0.7 %copy-done.5 = f32[2,2,320]{2,1,0:T(2,128)S(1)} copy-done((f32[2,2,320]{2,1,0:T(2,128)S(1)}, f32[2,2,320]{2,1,0:T(2,128)}, u32[]{:S(2)}) %copy-start.5) | copy-done | bytes 5144
  0.7 0.0 copy-start.6
  0.7 0.7 %copy-done.6 = f32[2,2,320]{2,1,0:T(2,128)S(1)} copy-done((f32[2,2,320]{2,1,0:T(2,128)S(1)}, f32[2,2,320]{2,1,0:T(2,128)}, u32[]{:S(2)}) %copy-start.6) | copy-done | bytes 5144
  1.4 0.0 copy-start
  1.4 1.2 %copy-done = bf16[2,2,3,960,40]{3,4,2,1,0:T(8,128)(2,1)S(1)} copy-done((bf16[2,2,3,960,40]{3,4,2,1,0:T(8,128)(2,1)S(1)}, bf16[2,2,3,960,40]{3,4,2,1,0:T(8,128)(2,1)}, u32[]{:S(2)}) %copy-start) | copy-done | bytes 921624
  2.6 0.0 copy-start.1
  2.6 1.2 %copy-done.1 = bf16[2,1,6,96,320]{4,3,2,1,0:T(8,128)(2,1)S(1)} copy-done((bf16[2,1,6,96,320]{4,3,2,1,0:T(8,128)(2,1)S(1)}, bf16[2,1,6,96,320]{4,3,2,1,0:T(8,128)(2,1)}, u32[]{:S(2)}) %copy-start.1) | copy-done | bytes 737304
  3.8 0.0 copy-start.2
  3.8 1.0 %copy-done.2 = f32[320,320]{1,0:T(8,128)S(1)} copy-done((f32[320,320]{1,0:T(8,128)S(1)}, f32[320,320]{1,0:T(8,128)}, u32[]{:S(2)}) %copy-start.2) | copy-done | bytes 409624
  4.8 0.0 copy-start.3
  4.8 1.0 %copy-done.3 = bf16[1,6,96,320]{3,2,1,0:T(8,128)(2,1)S(1)} copy-done((bf16[1,6,96,320]{3,2,1,0:T(8,128)(2,1)S(1)}, bf16[1,6,96,320]{3,2,1,0:T(8,128)(2,1)}, u32[]{:S(2)}) %copy-start.3) | copy-done | bytes 368664
  5.8 0.0 copy-start.4
  5.8 0.8 %copy-done.4 = bf16[2,1,320,40]{2,3,1,0:T(8,128)(2,1)S(1)} copy-done((bf16[2,1,320,40]{2,3,1,0:T(8,128)(2,1)S(1)}, bf16[2,1,320,40]{2,3,1,0:T(8,128)(2,1)}, u32[]{:S(2)}) %copy-start.4) | copy-done | bytes 51224
  6.6 56.5 %shard_map.73 = bf16[2,576,320]{2,1,0:T(8,128)(2,1)S(1)} custom-call(bf16[576,320]{1,0:T(8,128)(2,1)S(1)} %bitcast.14, bf16[2,576,320]{2,1,0:T(8,128)(2,1)S(1)} %bitcast.13, f32[4,320]{1,0:T(4,128)S(1)} %reshape.20.gain_ref, f32[4,320]{1,0:T(4,128)S(1)} %reshape.21.shift_ref, f32[320,320]{1,0:T(8,128)S(1)} %copy-done.2, bf16[4,120,960]{2,1,0:T(8,128)(2,1)S(1)} %bitcast.12, ...), custom_call_target="tpu_custom_call" | custom-call | tf_op jit(solution)/shard_map/pallas_call | solution.py:318
  63.2 0.9 %copy.10 = bf16[2,1,6,96,320]{4,3,2,1,0:T(8,128)(2,1)} copy(bf16[2,1,6,96,320]{4,3,2,1,0:T(8,128)(2,1)S(1)} %bitcast.11) | data formatting | bytes 1474560
  (2 shorter events, 0.0 us)
Async XLA Ops:
  0.0 0.7 %copy-start.5 = (f32[2,2,320]{2,1,0:T(2,128)S(1)}, f32[2,2,320]{2,1,0:T(2,128)}, u32[]{:S(2)}) copy-start(f32[2,2,320]{2,1,0:T(2,128)} %param.9) | copy-start | bytes 15364
  0.7 0.7 %copy-start.6 = (f32[2,2,320]{2,1,0:T(2,128)S(1)}, f32[2,2,320]{2,1,0:T(2,128)}, u32[]{:S(2)}) copy-start(f32[2,2,320]{2,1,0:T(2,128)} %param.10) | copy-start | bytes 15364
  1.4 1.2 %copy-start = (bf16[2,2,3,960,40]{3,4,2,1,0:T(8,128)(2,1)S(1)}, bf16[2,2,3,960,40]{3,4,2,1,0:T(8,128)(2,1)}, u32[]{:S(2)}) copy-start(bf16[2,2,3,960,40]{3,4,2,1,0:T(8,128)(2,1)} %param.11) | copy-start | bytes 2764804
  2.6 1.2 %copy-start.1 = (bf16[2,1,6,96,320]{4,3,2,1,0:T(8,128)(2,1)S(1)}, bf16[2,1,6,96,320]{4,3,2,1,0:T(8,128)(2,1)}, u32[]{:S(2)}) copy-start(bf16[2,1,6,96,320]{4,3,2,1,0:T(8,128)(2,1)} %param.8) | copy-start | bytes 2211844
  3.8 1.0 %copy-start.2 = (f32[320,320]{1,0:T(8,128)S(1)}, f32[320,320]{1,0:T(8,128)}, u32[]{:S(2)}) copy-start(f32[320,320]{1,0:T(8,128)} %constant.2.clone.group_ref) | copy-start | bytes 1228804
  4.8 1.0 %copy-start.3 = (bf16[1,6,96,320]{3,2,1,0:T(8,128)(2,1)S(1)}, bf16[1,6,96,320]{3,2,1,0:T(8,128)(2,1)}, u32[]{:S(2)}) copy-start(bf16[1,6,96,320]{3,2,1,0:T(8,128)(2,1)} %param.7) | copy-start | bytes 1105924
  5.8 0.8 %copy-start.4 = (bf16[2,1,320,40]{2,3,1,0:T(8,128)(2,1)S(1)}, bf16[2,1,320,40]{2,3,1,0:T(8,128)(2,1)}, u32[]{:S(2)}) copy-start(bf16[2,1,320,40]{2,3,1,0:T(8,128)(2,1)} %param.12) | copy-start | bytes 153604
where the time goes:
time: 64.5 us; the launch traced here: 64.1 us
  Pallas kernels  56.5 us (88%)
  local copies, waits for them, and re-layouts  7.54 us (12%)
    pallas_call x1, Pallas kernels, on_device(): pl.pallas_call(functools.partial(kernel, dims), out_shape=jax.ShapeDtypeS...  56.5 us
    unnamed x15, local copies, waits for them, and re-layouts  7.51 us

commit v1 on v0

v1 whole, which is shorter than its diff:
```python
import functools

import jax
import jax.numpy as jnp
from jax import lax
from jax.experimental import pallas as pl
from jax.experimental.pallas import tpu as pltpu
from jax.sharding import PartitionSpec as P

GROUPS = 32
EPSILON = 1e-05
MESH = pl.DeviceIdType.MESH
LOOKAHEAD = 3
TO_B, TO_D = 2, 4


def transposed(conv_weights, zero_weights):
    blocks, convs, taps, depth, outs = conv_weights.shape
    conv = jnp.transpose(conv_weights, (0, 1, 2, 4, 3)).reshape(blocks * convs * taps, outs, depth)
    return conv, jnp.transpose(zero_weights[:, 0], (0, 2, 1))


def kernel(dims, x_hbm, skip_hbm, gain_hbm, shift_hbm, w_hbm, zw_hbm, out_ref,
           xv, skipv, gainv, shiftv, wv, zwv, group, slabs, wfull, zfull, stk, acc, halo, fields,
           stat_out, stat_in, load,
           z_send, z_recv, a_send, a_recv, b_send, b_recv, d_send, d_recv,
           h_send, h_recv, t_send, t_recv):
    rows_n, batch_n, height, across, channels, outs, taps, members = dims
    units, _, depth = w_hbm.shape
    blocks = zw_hbm.shape[0]
    convs = units // taps
    per_block = convs // blocks
    lanes = slabs.shape[3]
    piece = lanes - depth
    pieces = -(-channels // piece)
    cells = height * across
    zn = batch_n // 2
    r = lax.axis_index("rows")
    b = lax.axis_index("batch")
    z, c = b // 2, b % 2
    bit0, bit1 = r % 2, (r // 2) % 2
    px, py = r + 1 - 2 * bit0, r + 2 - 4 * bit1
    mate = b + 1 - 2 * c
    quarter, eighth = lanes // 4, lanes // 8
    g = bit0 * (1 + bit1) + (1 - bit0) * 3 * bit1
    gx = g + 1 - 2 * (g % 2)
    gy = 3 - g
    even = (g + g % 2) % 4
    odd = g + 1 - g % 2

    def part(index):
        return pl.ds(pl.multiple_of(index * quarter, quarter), quarter)

    def first(index):
        return pl.ds(pl.multiple_of(index * quarter, eighth), eighth)

    def second(index):
        return pl.ds(pl.multiple_of(index * quarter + eighth, eighth), eighth)

    def plane(m):
        other, weight = 0, 1
        while weight < zn:
            other = other + ((z // weight + m // weight) % 2) * weight
            weight *= 2
        return other

    def slab(m):
        return plane(m) * 2 + c

    far = list(range(zn - 1, 1, -1))

    def remote(src, dst, send, recv, row, batch):
        return pltpu.make_async_remote_copy(
            src_ref=src, dst_ref=dst, send_sem=send, recv_sem=recv,
            device_id={"rows": row, "batch": batch}, device_id_type=MESH)

    barrier = pltpu.get_barrier_semaphore()
    for j in range(1, zn):
        pl.semaphore_signal(barrier, inc=1, device_id_type=MESH,
                            device_id={"rows": r, "batch": ((z + j) % zn) * 2 + c})
    for j in range(1, rows_n):
        pl.semaphore_signal(barrier, inc=1, device_id_type=MESH,
                            device_id={"rows": (r + j) % rows_n, "batch": b})
    pl.semaphore_signal(barrier, inc=1, device_id_type=MESH, device_id={"rows": r, "batch": mate})

    loads = [
        pltpu.make_async_copy(w_hbm.at[pl.ds(0, taps)], wv.at[pl.ds(0, taps)], load.at[0]),
        pltpu.make_async_copy(zw_hbm, zwv, load.at[1]),
        pltpu.make_async_copy(x_hbm, xv, load.at[2]),
        pltpu.make_async_copy(w_hbm.at[pl.ds(taps, units - taps)], wv.at[pl.ds(taps, units - taps)],
                              load.at[3]),
        pltpu.make_async_copy(gain_hbm, gainv, load.at[4]),
        pltpu.make_async_copy(shift_hbm, shiftv, load.at[5]),
        pltpu.make_async_copy(skip_hbm, skipv, load.at[6]),
    ]
    for copy in loads:
        copy.start()

    def pack(u):
        block, p = u // (per_block * taps), u % (per_block * taps)
        slabs[u, b, :, :depth] = wv[u]
        if p < pieces:
            wide = min(piece, channels - p * piece)
            slabs[u, b, :, depth:depth + wide] = zwv[block, :, p * piece:p * piece + wide]

    def z_step(u):
        for m in far:
            here = slabs.at[u, b, :, part(g)]
            remote(here, here, z_send.at[u], z_recv.at[u], r, slab(m)).start()
        for index in (even, odd):
            here = slabs.at[u, b, :, part(index)]
            remote(here, here, z_send.at[u], z_recv.at[u], r, slab(1)).start()

    def own_step(u):
        here = slabs.at[u, b]
        remote(here, here, d_send.at[u], d_recv.at[u], r, mate).start()

    def totals(u):
        return (
            (slabs.at[u, pl.ds(0, zn), :, pl.ds(0, quarter)], z_send, z_recv),
            (slabs.at[u, pl.ds(0, zn - 1), :, pl.ds(0, 2 * quarter)], a_send, a_recv),
            (slabs.at[u, pl.ds(0, zn - 2), :, pl.ds(0, quarter)], b_send, b_recv),
            (slabs.at[u, pl.ds(0, zn)], d_send, d_recv),
        )

    def arrived(u, stage):
        ref, send, recv = totals(u)[stage]
        remote(ref, ref, send.at[u], recv.at[u], r, mate).wait_recv()

    def a_step(u):
        arrived(u, 0)
        for m in far:
            here = slabs.at[u, slab(m), :, part(g)]
            remote(here, here, a_send.at[u], a_recv.at[u], px, b).start()
            remote(here, here, a_send.at[u], a_recv.at[u], py, b).start()
        here = slabs.at[u, slab(1), :, part(even)]
        remote(here, here, a_send.at[u], a_recv.at[u], px, b).start()
        here = slabs.at[u, slab(1), :, part(odd)]
        remote(here, here, a_send.at[u], a_recv.at[u], py, b).start()

    def b_step(u):
        arrived(u, 1)
        for m in far:
            here = slabs.at[u, slab(m), :, first(gy)]
            remote(here, here, b_send.at[u], b_recv.at[u], px, b).start()
            here = slabs.at[u, slab(m), :, second(gx)]
            remote(here, here, b_send.at[u], b_recv.at[u], py, b).start()
        here = slabs.at[u, slab(1)]
        remote(here, here, d_send.at[u], d_recv.at[u], r, mate).start()

    def d_step(u):
        if far:
            arrived(u, 2)
        for m in far:
            here = slabs.at[u, slab(m)]
            remote(here, here, d_send.at[u], d_recv.at[u], r, mate).start()

    done = [0]

    def advance(count=1):
        for _ in range(min(count, units + TO_D - done[0])):
            j = done[0]
            done[0] += 1
            if 0 <= j - TO_D:
                d_step(j - TO_D)
            if 0 <= j - TO_B < units:
                b_step(j - TO_B)
            if j < units:
                a_step(j)
            if j + LOOKAHEAD < units:
                z_step(j + LOOKAHEAD)

    def assemble(u):
        arrived(u, 3)
        for d in range(batch_n):
            wfull[u % taps, d * outs:(d + 1) * outs, :] = slabs[u, d, :, :depth]

    def assemble_zero(block):
        for d in range(batch_n):
            parts = []
            for p in range(pieces):
                wide = min(piece, channels - p * piece)
                parts.append(slabs[block * per_block * taps + p, d, :, depth:depth + wide])
            zfull[d * outs:(d + 1) * outs, :] = jnp.concatenate(parts, axis=1)

    def times(a, w):
        return lax.dot_general(a, w, (((1,), (1,)), ((), ())), preferred_element_type=jnp.float32)

    def halo_copies(s, ref):
        def down():
            return remote(ref.at[pl.ds(cells - across, across)], halo.at[s, 0],
                          h_send.at[s, 0], h_recv.at[s, 0], (r + 1) % rows_n, b)

        def up():
            return remote(ref.at[pl.ds(0, across)], halo.at[s, 1],
                          h_send.at[s, 1], h_recv.at[s, 1], (r + rows_n - 1) % rows_n, b)

        return down, up

    def halo_start(s, ref):
        down, up = halo_copies(s, ref)

        @pl.when(r < rows_n - 1)
        def _():
            down().start()

        @pl.when(r > 0)
        def _():
            up().start()

        return down, up

    sent = []

    def stat_start(s, total, square):
        stat_out[s] = jnp.concatenate([total, square, jnp.zeros((6, channels), jnp.float32)], axis=0)
        for j in range(1, rows_n):
            copy = remote(stat_out.at[s], stat_in.at[s, j], t_send.at[s, j], t_recv.at[s, j],
                          (r + j) % rows_n, b)
            copy.start()
            sent.append(copy)

    col = lax.broadcasted_iota(jnp.int32, (across, channels), 0)

    def normalize(s, ref, ends):
        total = stat_out[s]
        for j in range(1, rows_n):
            here = stat_in.at[s, j]
            remote(here, here, t_send.at[s, j], t_recv.at[s, j], r, mate).wait_recv()
            total = total + stat_in[s, j]
        high = total.astype(jnp.bfloat16).astype(jnp.float32)
        rest = total - high
        middle = rest.astype(jnp.bfloat16).astype(jnp.float32)
        split = jnp.concatenate([high, middle, rest - middle], axis=0).astype(jnp.bfloat16)
        grouped = jnp.dot(split, group[...], preferred_element_type=jnp.float32)
        grouped = (grouped[0:8] + grouped[8:16] + grouped[16:24]) * (1.0 / members)
        mean = grouped[0:1]
        spread = jnp.maximum(grouped[1:2] - mean * mean, 0.0)
        block, half = s // per_block, s % per_block
        scale = lax.rsqrt(spread + EPSILON) * gainv[block, half:half + 1, :]
        bias = shiftv[block, half:half + 1, :] - mean * scale

        def put(at, v, valid):
            y = v.astype(jnp.float32) * scale + bias
            a = y / (1.0 + jnp.exp(-y))
            if valid is not None:
                a = jnp.where(valid, a, 0.0)
            left = jnp.where(col == 0, 0.0, pltpu.roll(a, 1, 0))
            right = jnp.where(col == across - 1, 0.0, pltpu.roll(a, across - 1, 0))
            stk[pl.ds(at, across), :] = jnp.concatenate(
                [left.astype(jnp.bfloat16), a.astype(jnp.bfloat16), right.astype(jnp.bfloat16)], axis=1)

        def body(i, carry):
            at = pl.multiple_of(i * across, across)
            put(pl.multiple_of(at + across, across), ref[pl.ds(at, across), :], None)
            return carry
        lax.fori_loop(0, height, body, 0)

        down, up = ends

        @pl.when(r > 0)
        def _():
            down().wait_recv()

        @pl.when(r < rows_n - 1)
        def _():
            up().wait_recv()

        put(0, halo[s, 0], r > 0)
        put((height + 1) * across, halo[s, 1], r < rows_n - 1)

    def keep(s, source, at, value):
        size = value.shape[0]
        if source is not None:
            value = source[at:at + size, :].astype(jnp.float32) + value
        value = value.astype(jnp.bfloat16)
        fields[s, at:at + size, :] = value
        kept = value.astype(jnp.float32)
        return (jnp.sum(kept, axis=0, keepdims=True),
                jnp.sum(kept * kept, axis=0, keepdims=True))

    def convolve(s, source):
        last = taps - 1
        for t in range(taps):
            advance(s * taps + t + TO_D + 1 - done[0])
            assemble(s * taps + t)
            if t == last:
                break
            value = times(stk[t * across:t * across + cells, :], wfull[t])
            acc[...] = value if t == 0 else acc[...] + value
            if t == 0:
                advance()
        low, high = last * across, (height - 1 + last) * across
        both = jnp.concatenate([stk[low:low + across, :], stk[high:high + across, :]], axis=0)
        border = times(both, wfull[last])
        top = keep(s, source, 0, acc[0:across, :] + border[:across])
        bottom = keep(s, source, cells - across, acc[cells - across:, :] + border[across:])
        if s + 1 < convs:
            ends.append(halo_start(s + 1, fields.at[s]))
        inner = times(stk[low + across:high, :], wfull[last])
        middle = keep(s, source, across, acc[across:cells - across, :] + inner)
        return middle[0] + top[0] + bottom[0], middle[1] + top[1] + bottom[1]

    def zero_conv(s):
        block = s // per_block
        assemble_zero(block)
        zeroed = times(fields[s], zfull[...])
        out_ref[block] = (skipv[block].astype(jnp.float32) + zeroed).astype(jnp.bfloat16)

    per = channels // GROUPS
    same = (lax.broadcasted_iota(jnp.int32, (channels, channels), 0) // per
            == lax.broadcasted_iota(jnp.int32, (channels, channels), 1) // per)
    group[...] = jnp.where(same, 1.0, 0.0).astype(jnp.bfloat16)

    loads[0].wait()
    loads[1].wait()
    for u in range(taps):
        pack(u)
    pl.semaphore_wait(barrier, zn + rows_n - 1)
    for u in range(min(LOOKAHEAD, units)):
        z_step(u)
        own_step(u)
    loads[2].wait()
    ends = [halo_start(0, xv)]
    whole = xv[...].astype(jnp.float32)
    stat_start(0, jnp.sum(whole, axis=0, keepdims=True), jnp.sum(whole * whole, axis=0, keepdims=True))
    loads[3].wait()
    for u in range(taps, units):
        pack(u)
    for u in range(min(LOOKAHEAD, units), units):
        own_step(u)
    for copy in loads[4:]:
        copy.wait()
    advance(1)
    normalize(0, xv, ends[0])
    advance(TO_D)
    source = xv
    for s in range(convs):
        if s > 0:
            advance()
            normalize(s, fields.at[s - 1], ends[s])
            advance()
        last = s % per_block == per_block - 1
        sums = convolve(s, source if last else None)
        if s < convs - 1:
            stat_start(s + 1, *sums)
        if last:
            source = fields.at[s]
            zero_conv(s)
    advance(units)
    for copy in sent:
        copy.wait_send()
    for u in range(units):
        for stage, (ref, send, recv) in enumerate(totals(u)):
            if far or stage != 2:
                remote(ref, ref, send.at[u], recv.at[u], r, mate).wait_send()
    for down, up in ends:
        @pl.when(r < rows_n - 1)
        def _():
            down().wait_send()

        @pl.when(r > 0)
        def _():
            up().wait_send()


def on_device(rows_n, batch_n, control, unet_skips, norm_gains, norm_shifts, conv_weights, zero_weights):
    blocks, convs, taps, depth, outs = conv_weights.shape
    samples, height, across, channels = control.shape
    lanes = (depth // 512 + 1) * 512
    stages = blocks * convs
    units = stages * taps
    cells = height * across
    per = channels // GROUPS
    conv, zero = transposed(conv_weights, zero_weights)
    members = cells * rows_n * per
    dims = (rows_n, batch_n, height, across, channels, outs, taps, members)
    dma = pltpu.SemaphoreType.DMA
    hbm = pl.BlockSpec(memory_space=pltpu.HBM)
    out = pl.pallas_call(
        functools.partial(kernel, dims),
        out_shape=jax.ShapeDtypeStruct((blocks, cells, channels), jnp.bfloat16),
        in_specs=[hbm] * 6,
        out_specs=pl.BlockSpec(memory_space=pltpu.VMEM),
        scratch_shapes=[
            pltpu.VMEM((cells, channels), jnp.bfloat16),
            pltpu.VMEM((blocks, cells, channels), jnp.bfloat16),
            pltpu.VMEM((blocks, convs, channels), jnp.float32),
            pltpu.VMEM((blocks, convs, channels), jnp.float32),
            pltpu.VMEM((units, outs, depth), jnp.bfloat16),
            pltpu.VMEM((blocks, outs, channels), jnp.bfloat16),
            pltpu.VMEM((channels, channels), jnp.bfloat16),
            pltpu.VMEM((units, batch_n, outs, lanes), jnp.bfloat16),
            pltpu.VMEM((taps, channels, depth), jnp.bfloat16),
            pltpu.VMEM((channels, channels), jnp.bfloat16),
            pltpu.VMEM(((height + taps - 1) * across, depth), jnp.bfloat16),
            pltpu.VMEM((cells, channels), jnp.float32),
            pltpu.VMEM((stages, 2, across, channels), jnp.bfloat16),
            pltpu.VMEM((stages, cells, channels), jnp.bfloat16),
            pltpu.VMEM((stages, 8, channels), jnp.float32),
            pltpu.VMEM((stages, rows_n, 8, channels), jnp.float32),
            dma((7,)),
            dma((units,)), dma((units,)),
            dma((units,)), dma((units,)),
            dma((units,)), dma((units,)),
            dma((units,)), dma((units,)),
            dma((stages, 2)), dma((stages, 2)),
            dma((stages, rows_n)), dma((stages, rows_n)),
        ],
        compiler_params=pltpu.CompilerParams(
            collective_id=0, has_side_effects=True, vmem_limit_bytes=50 * 1024 * 1024),
    )(
        control.reshape(cells, channels),
        unet_skips.reshape(blocks, cells, channels),
        norm_gains,
        norm_shifts,
        conv,
        zero,
    )
    return out.reshape(blocks, samples, height, across, channels)


def solution(mesh):
    placed = (
        P("batch", "rows", None, None),
        P(None, "batch", "rows", None, None),
        P(),
        P(),
        P(None, None, None, None, "batch"),
        P(None, None, None, "batch"),
    )
    return jax.shard_map(
        functools.partial(on_device, mesh.shape["rows"], mesh.shape["batch"]),
        mesh=mesh,
        in_specs=placed,
        out_specs=P(None, "batch", "rows", None, None),
        check_vma=False,
    )
```

time: 64.5 us -> 63.5 us (0.984)
  local copies, waits for them, and re-layouts: 7.54 us -> 6.51 us
    unnamed x15 -> x13, local copies, waits for them, and re-layouts: 7.51 us -> 6.51 us
where the time goes in v1:
time: 63.5 us; the launch traced here: 63 us
  Pallas kernels  56.5 us (89%)
  local copies, waits for them, and re-layouts  6.51 us (10%)
    pallas_call x1, Pallas kernels, on_device(): pl.pallas_call(functools.partial(kernel, dims), out_shape=jax.ShapeDtypeS...  56.5 us
    unnamed x13, local copies, waits for them, and re-layouts  6.51 us

profile of v1, /device:TPU:0, one launch (start us, length us, event | category | flops | bytes accessed | tf_op | source)
XLA Modules:
  0.0 63.0 jit_solution(1173225436025678320)
XLA Ops:
  0.0 0.0 copy-start.4
  0.0 0.7 %copy-done.4 = f32[2,2,320]{2,1,0:T(2,128)S(1)} copy-done((f32[2,2,320]{2,1,0:T(2,128)S(1)}, f32[2,2,320]{2,1,0:T(2,128)}, u32[]{:S(2)}) %copy-start.4) | copy-done | bytes 5144
  0.7 0.0 copy-start
  0.7 1.2 %copy-done = bf16[2,2,3,960,40]{3,4,2,1,0:T(8,128)(2,1)S(1)} copy-done((bf16[2,2,3,960,40]{3,4,2,1,0:T(8,128)(2,1)S(1)}, bf16[2,2,3,960,40]{3,4,2,1,0:T(8,128)(2,1)}, u32[]{:S(2)}) %copy-start) | copy-done | bytes 921624
  1.9 0.0 copy-start.1
  1.9 1.2 %copy-done.1 = bf16[2,1,6,96,320]{4,3,2,1,0:T(8,128)(2,1)S(1)} copy-done((bf16[2,1,6,96,320]{4,3,2,1,0:T(8,128)(2,1)S(1)}, bf16[2,1,6,96,320]{4,3,2,1,0:T(8,128)(2,1)}, u32[]{:S(2)}) %copy-start.1) | copy-done | bytes 737304
  3.1 0.0 copy-start.2
  3.1 1.0 %copy-done.2 = bf16[1,6,96,320]{3,2,1,0:T(8,128)(2,1)S(1)} copy-done((bf16[1,6,96,320]{3,2,1,0:T(8,128)(2,1)S(1)}, bf16[1,6,96,320]{3,2,1,0:T(8,128)(2,1)}, u32[]{:S(2)}) %copy-start.2) | copy-done | bytes 368664
  4.1 0.0 copy-start.3
  4.1 0.8 %copy-done.3 = bf16[2,1,320,40]{2,3,1,0:T(8,128)(2,1)S(1)} copy-done((bf16[2,1,320,40]{2,3,1,0:T(8,128)(2,1)S(1)}, bf16[2,1,320,40]{2,3,1,0:T(8,128)(2,1)}, u32[]{:S(2)}) %copy-start.3) | copy-done | bytes 51224
  4.9 0.0 copy-start.5
  4.9 0.7 %copy-done.5 = f32[2,2,320]{2,1,0:T(2,128)S(1)} copy-done((f32[2,2,320]{2,1,0:T(2,128)S(1)}, f32[2,2,320]{2,1,0:T(2,128)}, u32[]{:S(2)}) %copy-start.5) | copy-done | bytes 5144
  5.6 56.5 %shard_map.64 = bf16[2,576,320]{2,1,0:T(8,128)(2,1)S(1)} custom-call(bf16[576,320]{1,0:T(8,128)(2,1)S(1)} %bitcast.14, bf16[2,576,320]{2,1,0:T(8,128)(2,1)S(1)} %bitcast.13, f32[2,2,320]{2,1,0:T(2,128)S(1)} %copy-done.4, f32[2,2,320]{2,1,0:T(2,128)S(1)} %copy-done.5, bf16[12,40,960]{2,1,0:T(8,128)(2,1)S(1)} %bitcast.12, bf16[2,40,320]{2,1,0:T(8,128)(2,1)S(1)} %bitcast.15), custom_call_target="tpu_custom_call" | custom-call | tf_op jit(solution)/shard_map/pallas_call | solution.py:380
  62.1 0.9 %copy.9 = bf16[2,1,6,96,320]{4,3,2,1,0:T(8,128)(2,1)} copy(bf16[2,1,6,96,320]{4,3,2,1,0:T(8,128)(2,1)S(1)} %bitcast.11) | data formatting | bytes 1474560
Async XLA Ops:
  0.0 0.7 %copy-start.4 = (f32[2,2,320]{2,1,0:T(2,128)S(1)}, f32[2,2,320]{2,1,0:T(2,128)}, u32[]{:S(2)}) copy-start(f32[2,2,320]{2,1,0:T(2,128)} %gain_hbm.1) | copy-start | bytes 15364
  0.7 1.2 %copy-start = (bf16[2,2,3,960,40]{3,4,2,1,0:T(8,128)(2,1)S(1)}, bf16[2,2,3,960,40]{3,4,2,1,0:T(8,128)(2,1)}, u32[]{:S(2)}) copy-start(bf16[2,2,3,960,40]{3,4,2,1,0:T(8,128)(2,1)} %param.10) | copy-start | bytes 2764804
  1.9 1.2 %copy-start.1 = (bf16[2,1,6,96,320]{4,3,2,1,0:T(8,128)(2,1)S(1)}, bf16[2,1,6,96,320]{4,3,2,1,0:T(8,128)(2,1)}, u32[]{:S(2)}) copy-start(bf16[2,1,6,96,320]{4,3,2,1,0:T(8,128)(2,1)} %param.7) | copy-start | bytes 2211844
  3.1 1.0 %copy-start.2 = (bf16[1,6,96,320]{3,2,1,0:T(8,128)(2,1)S(1)}, bf16[1,6,96,320]{3,2,1,0:T(8,128)(2,1)}, u32[]{:S(2)}) copy-start(bf16[1,6,96,320]{3,2,1,0:T(8,128)(2,1)} %param.6) | copy-start | bytes 1105924
  4.1 0.8 %copy-start.3 = (bf16[2,1,320,40]{2,3,1,0:T(8,128)(2,1)S(1)}, bf16[2,1,320,40]{2,3,1,0:T(8,128)(2,1)}, u32[]{:S(2)}) copy-start(bf16[2,1,320,40]{2,3,1,0:T(8,128)(2,1)} %param.11) | copy-start | bytes 153604
  4.9 0.7 %copy-start.5 = (f32[2,2,320]{2,1,0:T(2,128)S(1)}, f32[2,2,320]{2,1,0:T(2,128)}, u32[]{:S(2)}) copy-start(f32[2,2,320]{2,1,0:T(2,128)} %shift_hbm.1) | copy-start | bytes 15364

commit v2 on v1

--- a/solution.py
+++ b/solution.py
@@ -222,7 +222,7 @@
 
     col = lax.broadcasted_iota(jnp.int32, (across, channels), 0)
 
-    def normalize(s, ref, ends):
+    def normalize(s, ref):
         total = stat_out[s]
         for j in range(1, rows_n):
             here = stat_in.at[s, j]
@@ -256,7 +256,10 @@
             return carry
         lax.fori_loop(0, height, body, 0)
 
-        down, up = ends
+        return put
+
+    def edges(s, put):
+        down, up = ends[s]
 
         @pl.when(r > 0)
         def _():
@@ -279,26 +282,36 @@
         return (jnp.sum(kept, axis=0, keepdims=True),
                 jnp.sum(kept * kept, axis=0, keepdims=True))
 
-    def convolve(s, source):
-        last = taps - 1
+    def convolve(s, source, put):
+        units_of = range(s * taps, (s + 1) * taps)
+        rows = cells - 2 * across
+        if s == 0:
+            for t, u in enumerate(units_of):
+                advance(u + TO_D + 1 - done[0])
+                assemble(u)
+                value = times(stk[(t + 1) * across:(t + 1) * across + rows, :], wfull[t])
+                if t < taps - 1:
+                    acc[...] = value if t == 0 else acc[...] + value
+            inner = acc[...] + value
+        else:
+            for u in units_of:
+                advance(u + TO_D + 1 - done[0])
+                assemble(u)
+            inner = None
+            for t in range(taps):
+                value = times(stk[(t + 1) * across:(t + 1) * across + rows, :], wfull[t])
+                inner = value if t == 0 else inner + value
+        middle = keep(s, source, across, inner)
+        advance()
+        edges(s, put)
+        border = None
         for t in range(taps):
-            advance(s * taps + t + TO_D + 1 - done[0])
-            assemble(s * taps + t)
-            if t == last:
-                break
-            value = times(stk[t * across:t * across + cells, :], wfull[t])
-            acc[...] = value if t == 0 else acc[...] + value
-            if t == 0:
-                advance()
-        low, high = last * across, (height - 1 + last) * across
-        both = jnp.concatenate([stk[low:low + across, :], stk[high:high + across, :]], axis=0)
-        border = times(both, wfull[last])
-        top = keep(s, source, 0, acc[0:across, :] + border[:across])
-        bottom = keep(s, source, cells - across, acc[cells - across:, :] + border[across:])
-        if s + 1 < convs:
-            ends.append(halo_start(s + 1, fields.at[s]))
-        inner = times(stk[low + across:high, :], wfull[last])
-        middle = keep(s, source, across, acc[across:cells - across, :] + inner)
+            low, high = t * across, (height - 1 + t) * across
+            both = jnp.concatenate([stk[low:low + across, :], stk[high:high + across, :]], axis=0)
+            value = times(both, wfull[t])
+            border = value if t == 0 else border + value
+        top = keep(s, source, 0, border[:across])
+        bottom = keep(s, source, cells - across, border[across:])
         return middle[0] + top[0] + bottom[0], middle[1] + top[1] + bottom[1]
 
     def zero_conv(s):
@@ -312,6 +325,9 @@
             == lax.broadcasted_iota(jnp.int32, (channels, channels), 1) // per)
     group[...] = jnp.where(same, 1.0, 0.0).astype(jnp.bfloat16)
 
+    loads[2].wait()
+    whole = xv[...].astype(jnp.float32)
+    sums = (jnp.sum(whole, axis=0, keepdims=True), jnp.sum(whole * whole, axis=0, keepdims=True))
     loads[0].wait()
     loads[1].wait()
     for u in range(taps):
@@ -319,11 +335,10 @@
     pl.semaphore_wait(barrier, zn + rows_n - 1)
     for u in range(min(LOOKAHEAD, units)):
         z_step(u)
+    stat_start(0, *sums)
+    ends = [halo_start(0, xv)]
+    for u in range(min(LOOKAHEAD, units)):
         own_step(u)
-    loads[2].wait()
-    ends = [halo_start(0, xv)]
-    whole = xv[...].astype(jnp.float32)
-    stat_start(0, jnp.sum(whole, axis=0, keepdims=True), jnp.sum(whole * whole, axis=0, keepdims=True))
     loads[3].wait()
     for u in range(taps, units):
         pack(u)
@@ -331,19 +346,18 @@
         own_step(u)
     for copy in loads[4:]:
         copy.wait()
-    advance(1)
-    normalize(0, xv, ends[0])
-    advance(TO_D)
+    put = normalize(0, xv)
+    advance(TO_D + 1)
     source = xv
     for s in range(convs):
         if s > 0:
-            advance()
-            normalize(s, fields.at[s - 1], ends[s])
-            advance()
+            advance(2)
+            put = normalize(s, fields.at[s - 1])
         last = s % per_block == per_block - 1
-        sums = convolve(s, source if last else None)
+        sums = convolve(s, source if last else None, put)
         if s < convs - 1:
             stat_start(s + 1, *sums)
+            ends.append(halo_start(s + 1, fields.at[s]))
         if last:
             source = fields.at[s]
             zero_conv(s)
@@ -394,7 +408,7 @@
             pltpu.VMEM((taps, channels, depth), jnp.bfloat16),
             pltpu.VMEM((channels, channels), jnp.bfloat16),
             pltpu.VMEM(((height + taps - 1) * across, depth), jnp.bfloat16),
-            pltpu.VMEM((cells, channels), jnp.float32),
+            pltpu.VMEM((cells - 2 * across, channels), jnp.float32),
             pltpu.VMEM((stages, 2, across, channels), jnp.bfloat16),
             pltpu.VMEM((stages, cells, channels), jnp.bfloat16),
             pltpu.VMEM((stages, 8, channels), jnp.float32),
@@ -408,7 +422,7 @@
             dma((stages, rows_n)), dma((stages, rows_n)),
         ],
         compiler_params=pltpu.CompilerParams(
-            collective_id=0, has_side_effects=True, vmem_limit_bytes=50 * 1024 * 1024),
+            collective_id=0, has_side_effects=True, vmem_limit_bytes=60 * 1024 * 1024),
     )(
         control.reshape(cells, channels),
         unet_skips.reshape(blocks, cells, channels),

time: 63.5 us -> 54.2 us (0.85)
  Pallas kernels: 56.5 us -> 51.8 us
  local copies, waits for them, and re-layouts: 6.51 us -> 2.17 us
    pallas_call x1, Pallas kernels: 56.5 us -> 51.8 us  [on_device(): pl.pallas_call(functools.partial(kernel, dims), out_shape=jax.ShapeDtypeS...]
    unnamed x13 -> x1, local copies, waits for them, and re-layouts: 6.51 us -> 2.17 us
where the time goes in v2:
time: 54.2 us; the launch traced here: 54 us
  Pallas kernels  51.8 us (96%)
  local copies, waits for them, and re-layouts  2.17 us (4%)
    pallas_call x1, Pallas kernels, on_device(): pl.pallas_call(functools.partial(kernel, dims), out_shape=jax.ShapeDtypeS...  51.8 us
    unnamed x1, local copies, waits for them, and re-layouts  2.17 us

profile of v2, /device:TPU:0, one launch (start us, length us, event | category | flops | bytes accessed | tf_op | source)
XLA Modules:
  0.0 54.0 jit_solution(6782690611831593239)
XLA Ops:
  0.0 51.8 %shard_map.64 = bf16[2,576,320]{2,1,0:T(8,128)(2,1)} custom-call(bf16[576,320]{1,0:T(8,128)(2,1)} %bitcast.14, bf16[2,576,320]{2,1,0:T(8,128)(2,1)} %bitcast.13, f32[2,2,320]{2,1,0:T(2,128)} %gain_hbm.1, f32[2,2,320]{2,1,0:T(2,128)} %shift_hbm.1, bf16[12,40,960]{2,1,0:T(8,128)(2,1)} %bitcast.12, bf16[2,40,320]{2,1,0:T(8,128)(2,1)} %bitcast.15), custom_call_target="tpu_custom_call" | custom-call | tf_op jit(solution)/shard_map/pallas_call | solution.py:394
  51.9 2.2 %copy.9 = bf16[2,1,6,96,320]{4,3,2,1,0:T(8,128)(2,1)} copy(bf16[2,1,6,96,320]{4,3,2,1,0:T(8,128)(2,1)} %bitcast.11) | data formatting | bytes 1474560

commit v3 on v2

--- a/solution.py
+++ b/solution.py
@@ -10,8 +10,21 @@
 GROUPS = 32
 EPSILON = 1e-05
 MESH = pl.DeviceIdType.MESH
-LOOKAHEAD = 3
-TO_B, TO_D = 2, 4
+LOOKAHEAD = 4
+DIRECT = (2,)
+PLAN = {
+    "start": "A0 A1 B0 A2 B1 A3 D0 A4 B2 A5",
+    "tap0": "D1 B3",
+    "tap1": "B4",
+    "tail0": "B5",
+    "wait0": "A6 A7 D3 D4",
+    "norm1": "D5 A8 B6",
+    "half1": "B7 A9",
+    "wait1": "A10 D6 B8 A11 D7 B9",
+    "norm2": "D8 B10",
+    "half2": "D9 B11",
+    "wait2": "D10 D11",
+}
 
 
 def transposed(conv_weights, zero_weights):
@@ -40,6 +53,7 @@
     z, c = b // 2, b % 2
     bit0, bit1 = r % 2, (r // 2) % 2
     px, py = r + 1 - 2 * bit0, r + 2 - 4 * bit1
+    pxy = px + py - r
     mate = b + 1 - 2 * c
     quarter, eighth = lanes // 4, lanes // 8
     g = bit0 * (1 + bit1) + (1 - bit0) * 3 * bit1
@@ -83,11 +97,12 @@
                             device_id={"rows": (r + j) % rows_n, "batch": b})
     pl.semaphore_signal(barrier, inc=1, device_id_type=MESH, device_id={"rows": r, "batch": mate})
 
+    ahead = min(LOOKAHEAD, units - 1)
     loads = [
-        pltpu.make_async_copy(w_hbm.at[pl.ds(0, taps)], wv.at[pl.ds(0, taps)], load.at[0]),
+        pltpu.make_async_copy(w_hbm.at[pl.ds(0, ahead)], wv.at[pl.ds(0, ahead)], load.at[0]),
         pltpu.make_async_copy(zw_hbm, zwv, load.at[1]),
         pltpu.make_async_copy(x_hbm, xv, load.at[2]),
-        pltpu.make_async_copy(w_hbm.at[pl.ds(taps, units - taps)], wv.at[pl.ds(taps, units - taps)],
+        pltpu.make_async_copy(w_hbm.at[pl.ds(ahead, units - ahead)], wv.at[pl.ds(ahead, units - ahead)],
                               load.at[3]),
         pltpu.make_async_copy(gain_hbm, gainv, load.at[4]),
         pltpu.make_async_copy(shift_hbm, shiftv, load.at[5]),
@@ -118,7 +133,8 @@
     def totals(u):
         return (
             (slabs.at[u, pl.ds(0, zn), :, pl.ds(0, quarter)], z_send, z_recv),
-            (slabs.at[u, pl.ds(0, zn - 1), :, pl.ds(0, 2 * quarter)], a_send, a_recv),
+            (slabs.at[u, pl.ds(0, 3 * zn // 2 - 2 if u in DIRECT else zn - 1), :, pl.ds(0, 2 * quarter)],
+             a_send, a_recv),
             (slabs.at[u, pl.ds(0, zn - 2), :, pl.ds(0, quarter)], b_send, b_recv),
             (slabs.at[u, pl.ds(0, zn)], d_send, d_recv),
         )
@@ -133,6 +149,8 @@
             here = slabs.at[u, slab(m), :, part(g)]
             remote(here, here, a_send.at[u], a_recv.at[u], px, b).start()
             remote(here, here, a_send.at[u], a_recv.at[u], py, b).start()
+            if u in DIRECT:
+                remote(here, here, a_send.at[u], a_recv.at[u], pxy, b).start()
         here = slabs.at[u, slab(1), :, part(even)]
         remote(here, here, a_send.at[u], a_recv.at[u], px, b).start()
         here = slabs.at[u, slab(1), :, part(odd)]
@@ -140,35 +158,60 @@
 
     def b_step(u):
         arrived(u, 1)
-        for m in far:
-            here = slabs.at[u, slab(m), :, first(gy)]
-            remote(here, here, b_send.at[u], b_recv.at[u], px, b).start()
-            here = slabs.at[u, slab(m), :, second(gx)]
-            remote(here, here, b_send.at[u], b_recv.at[u], py, b).start()
+        if u in DIRECT:
+            for m in far:
+                here = slabs.at[u, slab(m)]
+                remote(here, here, d_send.at[u], d_recv.at[u], r, mate).start()
+        elif far:
+            @pl.when(bit0 == bit1)
+            def _():
+                for m in far:
+                    here = slabs.at[u, slab(m), :, first(gy)]
+                    remote(here, here, b_send.at[u], b_recv.at[u], px, b).start()
+                    here = slabs.at[u, slab(m), :, second(gx)]
+                    remote(here, here, b_send.at[u], b_recv.at[u], py, b).start()
+
+            @pl.when(bit0 != bit1)
+            def _():
+                for m in far:
+                    here = slabs.at[u, slab(m), :, part(gx)]
+                    remote(here, here, b_send.at[u], b_recv.at[u], py, b).start()
         here = slabs.at[u, slab(1)]
         remote(here, here, d_send.at[u], d_recv.at[u], r, mate).start()
 
     def d_step(u):
+        if u in DIRECT:
+            return
         if far:
             arrived(u, 2)
         for m in far:
             here = slabs.at[u, slab(m)]
             remote(here, here, d_send.at[u], d_recv.at[u], r, mate).start()
 
-    done = [0]
-
-    def advance(count=1):
-        for _ in range(min(count, units + TO_D - done[0])):
-            j = done[0]
-            done[0] += 1
-            if 0 <= j - TO_D:
-                d_step(j - TO_D)
-            if 0 <= j - TO_B < units:
-                b_step(j - TO_B)
-            if j < units:
-                a_step(j)
-            if j + LOOKAHEAD < units:
-                z_step(j + LOOKAHEAD)
+    stages = {"A": a_step, "B": b_step, "D": d_step}
+    done = set()
+
+    def step(kind, u):
+        if u >= units or (kind, u) in done:
+            return
+        for before in "ABD"[:"ABD".index(kind)]:
+            step(before, u)
+        if kind != "A" and u > 0:
+            step(kind, u - 1)
+        elif u > 0:
+            step("A", u - 1)
+        done.add((kind, u))
+        stages[kind](u)
+        if kind == "A" and u + ahead < units:
+            z_step(u + ahead)
+            own_step(u + ahead)
+
+    def plan(place):
+        for item in PLAN.get(place, "").split():
+            step(item[0], int(item[1:]))
+
+    def need(u):
+        step("B" if u in DIRECT else "D", u)
 
     def assemble(u):
         arrived(u, 3)
@@ -286,23 +329,23 @@
         units_of = range(s * taps, (s + 1) * taps)
         rows = cells - 2 * across
         if s == 0:
+            edges(s, put)
             for t, u in enumerate(units_of):
-                advance(u + TO_D + 1 - done[0])
+                need(u)
                 assemble(u)
-                value = times(stk[(t + 1) * across:(t + 1) * across + rows, :], wfull[t])
+                value = times(stk[t * across:t * across + cells, :], wfull[t])
                 if t < taps - 1:
                     acc[...] = value if t == 0 else acc[...] + value
-            inner = acc[...] + value
-        else:
-            for u in units_of:
-                advance(u + TO_D + 1 - done[0])
-                assemble(u)
-            inner = None
-            for t in range(taps):
-                value = times(stk[(t + 1) * across:(t + 1) * across + rows, :], wfull[t])
-                inner = value if t == 0 else inner + value
+                    plan(f"tap{t}")
+            return keep(s, source, 0, acc[...] + value)
+        inner = None
+        for t, u in enumerate(units_of):
+            need(u)
+            assemble(u)
+            value = times(stk[(t + 1) * across:(t + 1) * across + rows, :], wfull[t])
+            inner = value if t == 0 else inner + value
         middle = keep(s, source, across, inner)
-        advance()
+        plan(f"half{s}")
         edges(s, put)
         border = None
         for t in range(taps):
@@ -330,43 +373,43 @@
     sums = (jnp.sum(whole, axis=0, keepdims=True), jnp.sum(whole * whole, axis=0, keepdims=True))
     loads[0].wait()
     loads[1].wait()
-    for u in range(taps):
+    for u in range(ahead):
         pack(u)
     pl.semaphore_wait(barrier, zn + rows_n - 1)
-    for u in range(min(LOOKAHEAD, units)):
+    for u in range(ahead):
         z_step(u)
     stat_start(0, *sums)
     ends = [halo_start(0, xv)]
-    for u in range(min(LOOKAHEAD, units)):
+    for u in range(ahead):
         own_step(u)
     loads[3].wait()
-    for u in range(taps, units):
+    for u in range(ahead, units):
         pack(u)
-    for u in range(min(LOOKAHEAD, units), units):
-        own_step(u)
     for copy in loads[4:]:
         copy.wait()
     put = normalize(0, xv)
-    advance(TO_D + 1)
+    plan("start")
     source = xv
     for s in range(convs):
         if s > 0:
-            advance(2)
+            plan(f"wait{s - 1}")
             put = normalize(s, fields.at[s - 1])
+            plan(f"norm{s}")
         last = s % per_block == per_block - 1
         sums = convolve(s, source if last else None, put)
+        plan(f"tail{s}")
         if s < convs - 1:
             stat_start(s + 1, *sums)
             ends.append(halo_start(s + 1, fields.at[s]))
         if last:
             source = fields.at[s]
             zero_conv(s)
-    advance(units)
+    need(units - 1)
     for copy in sent:
         copy.wait_send()
     for u in range(units):
         for stage, (ref, send, recv) in enumerate(totals(u)):
-            if far or stage != 2:
+            if stage != 2 or far and u not in DIRECT:
                 remote(ref, ref, send.at[u], recv.at[u], r, mate).wait_send()
     for down, up in ends:
         @pl.when(r < rows_n - 1)
@@ -408,7 +451,7 @@
             pltpu.VMEM((taps, channels, depth), jnp.bfloat16),
             pltpu.VMEM((channels, channels), jnp.bfloat16),
             pltpu.VMEM(((height + taps - 1) * across, depth), jnp.bfloat16),
-            pltpu.VMEM((cells - 2 * across, channels), jnp.float32),
+            pltpu.VMEM((cells, channels), jnp.float32),
             pltpu.VMEM((stages, 2, across, channels), jnp.bfloat16),
             pltpu.VMEM((stages, cells, channels), jnp.bfloat16),
             pltpu.VMEM((stages, 8, channels), jnp.float32),
@@ -422,15 +465,15 @@
             dma((stages, rows_n)), dma((stages, rows_n)),
         ],
         compiler_params=pltpu.CompilerParams(
-            collective_id=0, has_side_effects=True, vmem_limit_bytes=60 * 1024 * 1024),
-    )(
+            collective_id=0, has_side_effects=True, vmem_limit_bytes=50 * 1024 * 1024),
+    )(*(pltpu.with_memory_space_constraint(array, pltpu.HBM) for array in (
         control.reshape(cells, channels),
         unet_skips.reshape(blocks, cells, channels),
         norm_gains,
         norm_shifts,
         conv,
         zero,
-    )
+    )))
     return out.reshape(blocks, samples, height, across, channels)
 
 

time: 54.2 us -> 52.4 us (0.967)
  local copies, waits for them, and re-layouts: 2.17 us -> 0.91 us
    unnamed x1, local copies, waits for them, and re-layouts: 2.17 us -> 0.91 us
where the time goes in v3:
time: 52.4 us; the launch traced here: 52.3 us
  Pallas kernels  51.3 us (98%)
  local copies, waits for them, and re-layouts  0.91 us (2%)
    pallas_call x1, Pallas kernels, on_device(): pl.pallas_call(functools.partial(kernel, dims), out_shape=jax.ShapeDtypeS...  51.3 us

profile of v3, /device:TPU:0, one launch (start us, length us, event | category | flops | bytes accessed | tf_op | source)
XLA Modules:
  0.0 52.3 jit_solution(16895160744722122448)
XLA Ops:
  0.0 51.3 %shard_map.64 = bf16[2,576,320]{2,1,0:T(8,128)(2,1)S(1)} custom-call(bf16[576,320]{1,0:T(8,128)(2,1)} %bitcast.14, bf16[2,576,320]{2,1,0:T(8,128)(2,1)} %bitcast.13, f32[2,2,320]{2,1,0:T(2,128)} %gain_hbm.1, f32[2,2,320]{2,1,0:T(2,128)} %shift_hbm.1, bf16[12,40,960]{2,1,0:T(8,128)(2,1)} %bitcast.12, bf16[2,40,320]{2,1,0:T(8,128)(2,1)} %bitcast.15), custom_call_target="tpu_custom_call" | custom-call | tf_op jit(solution)/shard_map/pallas_call | solution.py:437
  51.4 0.9 %copy.9 = bf16[2,1,6,96,320]{4,3,2,1,0:T(8,128)(2,1)} copy(bf16[2,1,6,96,320]{4,3,2,1,0:T(8,128)(2,1)S(1)} %bitcast.11) | data formatting | bytes 1474560

commit v4 on v3

--- a/solution.py
+++ b/solution.py
@@ -13,17 +13,19 @@
 LOOKAHEAD = 4
 DIRECT = (2,)
 PLAN = {
-    "start": "A0 A1 B0 A2 B1 A3 D0 A4 B2 A5",
-    "tap0": "D1 B3",
-    "tap1": "B4",
-    "tail0": "B5",
-    "wait0": "A6 A7 D3 D4",
-    "norm1": "D5 A8 B6",
-    "half1": "B7 A9",
-    "wait1": "A10 D6 B8 A11 D7 B9",
-    "norm2": "D8 B10",
-    "half2": "D9 B11",
-    "wait2": "D10 D11",
+    "start": ("A0", "A1", "B0", "A2", "B1", "A3", "D0", "A4"),
+    "pre0": ("B2", "A5", "D1"),
+    "tap0": ("B3",),
+    "tap1": ("B4",),
+    "stat0": ("B5",),
+    "wait0": ("A6", "D3", "A7", "D4", "A8", "D5", "A9"),
+    "half1": ("B6",),
+    "stat1": ("B7",),
+    "wait1": ("B8", "A10", "D6", "B9", "A11", "D7"),
+    "norm2": ("D8",),
+    "half2": ("B10", "D9"),
+    "wait2": ("B11", "D10"),
+    "norm3": ("D11",),
 }
 
 
@@ -207,7 +209,7 @@
             own_step(u + ahead)
 
     def plan(place):
-        for item in PLAN.get(place, "").split():
+        for item in PLAN.get(place, ()):
             step(item[0], int(item[1:]))
 
     def need(u):
@@ -336,6 +338,8 @@
                 value = times(stk[t * across:t * across + cells, :], wfull[t])
                 if t < taps - 1:
                     acc[...] = value if t == 0 else acc[...] + value
+                    if t == 0:
+                        plan("pre0")
                     plan(f"tap{t}")
             return keep(s, source, 0, acc[...] + value)
         inner = None
@@ -397,9 +401,9 @@
             plan(f"norm{s}")
         last = s % per_block == per_block - 1
         sums = convolve(s, source if last else None, put)
-        plan(f"tail{s}")
         if s < convs - 1:
             stat_start(s + 1, *sums)
+            plan(f"stat{s}")
             ends.append(halo_start(s + 1, fields.at[s]))
         if last:
             source = fields.at[s]

time: 52.4 us -> 49.7 us (0.948)
  Pallas kernels: 51.3 us -> 48.6 us
    pallas_call x1, Pallas kernels: 51.3 us -> 48.6 us  [on_device(): pl.pallas_call(functools.partial(kernel, dims), out_shape=jax.ShapeDtypeS...]
where the time goes in v4:
time: 49.7 us; the launch traced here: 49.6 us
  Pallas kernels  48.6 us (98%)
  local copies, waits for them, and re-layouts  0.91 us (2%)
    pallas_call x1, Pallas kernels, on_device(): pl.pallas_call(functools.partial(kernel, dims), out_shape=jax.ShapeDtypeS...  48.6 us

profile of v4, /device:TPU:0, one launch (start us, length us, event | category | flops | bytes accessed | tf_op | source)
XLA Modules:
  0.0 49.6 jit_solution(1720938279080016629)
XLA Ops:
  0.0 48.6 %shard_map.64 = bf16[2,576,320]{2,1,0:T(8,128)(2,1)S(1)} custom-call(bf16[576,320]{1,0:T(8,128)(2,1)} %bitcast.14, bf16[2,576,320]{2,1,0:T(8,128)(2,1)} %bitcast.13, f32[2,2,320]{2,1,0:T(2,128)} %gain_hbm.1, f32[2,2,320]{2,1,0:T(2,128)} %shift_hbm.1, bf16[12,40,960]{2,1,0:T(8,128)(2,1)} %bitcast.12, bf16[2,40,320]{2,1,0:T(8,128)(2,1)} %bitcast.15), custom_call_target="tpu_custom_call" | custom-call | tf_op jit(solution)/shard_map/pallas_call | solution.py:441
  48.6 0.9 %copy.9 = bf16[2,1,6,96,320]{4,3,2,1,0:T(8,128)(2,1)} copy(bf16[2,1,6,96,320]{4,3,2,1,0:T(8,128)(2,1)S(1)} %bitcast.11) | data formatting | bytes 1474560

commit v5 on v4

--- a/solution.py
+++ b/solution.py
@@ -14,17 +14,17 @@
 DIRECT = (2,)
 PLAN = {
     "start": ("A0", "A1", "B0", "A2", "B1", "A3", "D0", "A4"),
-    "pre0": ("B2", "A5", "D1"),
-    "tap0": ("B3",),
+    "half0": ("B2", "A5", "D1", "B3"),
     "tap1": ("B4",),
     "stat0": ("B5",),
-    "wait0": ("A6", "D3", "A7", "D4", "A8", "D5", "A9"),
-    "half1": ("B6",),
+    "wait0": ("A6", "D3", "A7", "D4", "A8", "D5"),
+    "edge1": ("B6",),
     "stat1": ("B7",),
-    "wait1": ("B8", "A10", "D6", "B9", "A11", "D7"),
+    "wait1": ("B8", "A9", "D6", "A10", "D7", "A11"),
     "norm2": ("D8",),
-    "half2": ("B10", "D9"),
-    "wait2": ("B11", "D10"),
+    "edge2": ("B9",),
+    "stat2": ("B10",),
+    "wait2": ("B11", "D9", "D10"),
     "norm3": ("D11",),
 }
 
@@ -84,6 +84,7 @@
         return plane(m) * 2 + c
 
     far = list(range(zn - 1, 1, -1))
+    order = [taps // 2] + [t for t in range(taps) if t != taps // 2]
 
     def remote(src, dst, send, recv, row, batch):
         return pltpu.make_async_remote_copy(
@@ -100,11 +101,12 @@
     pl.semaphore_signal(barrier, inc=1, device_id_type=MESH, device_id={"rows": r, "batch": mate})
 
     ahead = min(LOOKAHEAD, units - 1)
+    early = -(-ahead // taps) * taps
     loads = [
-        pltpu.make_async_copy(w_hbm.at[pl.ds(0, ahead)], wv.at[pl.ds(0, ahead)], load.at[0]),
+        pltpu.make_async_copy(w_hbm.at[pl.ds(0, early)], wv.at[pl.ds(0, early)], load.at[0]),
         pltpu.make_async_copy(zw_hbm, zwv, load.at[1]),
         pltpu.make_async_copy(x_hbm, xv, load.at[2]),
-        pltpu.make_async_copy(w_hbm.at[pl.ds(ahead, units - ahead)], wv.at[pl.ds(ahead, units - ahead)],
+        pltpu.make_async_copy(w_hbm.at[pl.ds(early, units - early)], wv.at[pl.ds(early, units - early)],
                               load.at[3]),
         pltpu.make_async_copy(gain_hbm, gainv, load.at[4]),
         pltpu.make_async_copy(shift_hbm, shiftv, load.at[5]),
@@ -115,7 +117,7 @@
 
     def pack(u):
         block, p = u // (per_block * taps), u % (per_block * taps)
-        slabs[u, b, :, :depth] = wv[u]
+        slabs[u, b, :, :depth] = wv[u // taps * taps + order[u % taps]]
         if p < pieces:
             wide = min(piece, channels - p * piece)
             slabs[u, b, :, depth:depth + wide] = zwv[block, :, p * piece:p * piece + wide]
@@ -123,14 +125,14 @@
     def z_step(u):
         for m in far:
             here = slabs.at[u, b, :, part(g)]
-            remote(here, here, z_send.at[u], z_recv.at[u], r, slab(m)).start()
+            remote(here, here, z_send.at[0], z_recv.at[u], r, slab(m)).start()
         for index in (even, odd):
             here = slabs.at[u, b, :, part(index)]
-            remote(here, here, z_send.at[u], z_recv.at[u], r, slab(1)).start()
+            remote(here, here, z_send.at[0], z_recv.at[u], r, slab(1)).start()
 
     def own_step(u):
         here = slabs.at[u, b]
-        remote(here, here, d_send.at[u], d_recv.at[u], r, mate).start()
+        remote(here, here, d_send.at[0], d_recv.at[u], r, mate).start()
 
     def totals(u):
         return (
@@ -143,43 +145,43 @@
 
     def arrived(u, stage):
         ref, send, recv = totals(u)[stage]
-        remote(ref, ref, send.at[u], recv.at[u], r, mate).wait_recv()
+        remote(ref, ref, send.at[0], recv.at[u], r, mate).wait_recv()
 
     def a_step(u):
         arrived(u, 0)
         for m in far:
             here = slabs.at[u, slab(m), :, part(g)]
-            remote(here, here, a_send.at[u], a_recv.at[u], px, b).start()
-            remote(here, here, a_send.at[u], a_recv.at[u], py, b).start()
+            remote(here, here, a_send.at[0], a_recv.at[u], px, b).start()
+            remote(here, here, a_send.at[0], a_recv.at[u], py, b).start()
             if u in DIRECT:
-                remote(here, here, a_send.at[u], a_recv.at[u], pxy, b).start()
+                remote(here, here, a_send.at[1], a_recv.at[u], pxy, b).start()
         here = slabs.at[u, slab(1), :, part(even)]
-        remote(here, here, a_send.at[u], a_recv.at[u], px, b).start()
+        remote(here, here, a_send.at[0], a_recv.at[u], px, b).start()
         here = slabs.at[u, slab(1), :, part(odd)]
-        remote(here, here, a_send.at[u], a_recv.at[u], py, b).start()
+        remote(here, here, a_send.at[0], a_recv.at[u], py, b).start()
 
     def b_step(u):
         arrived(u, 1)
         if u in DIRECT:
             for m in far:
                 here = slabs.at[u, slab(m)]
-                remote(here, here, d_send.at[u], d_recv.at[u], r, mate).start()
+                remote(here, here, d_send.at[0], d_recv.at[u], r, mate).start()
         elif far:
             @pl.when(bit0 == bit1)
             def _():
                 for m in far:
                     here = slabs.at[u, slab(m), :, first(gy)]
-                    remote(here, here, b_send.at[u], b_recv.at[u], px, b).start()
+                    remote(here, here, b_send.at[0], b_recv.at[u], px, b).start()
                     here = slabs.at[u, slab(m), :, second(gx)]
-                    remote(here, here, b_send.at[u], b_recv.at[u], py, b).start()
+                    remote(here, here, b_send.at[0], b_recv.at[u], py, b).start()
 
             @pl.when(bit0 != bit1)
             def _():
                 for m in far:
                     here = slabs.at[u, slab(m), :, part(gx)]
-                    remote(here, here, b_send.at[u], b_recv.at[u], py, b).start()
+                    remote(here, here, b_send.at[0], b_recv.at[u], py, b).start()
         here = slabs.at[u, slab(1)]
-        remote(here, here, d_send.at[u], d_recv.at[u], r, mate).start()
+        remote(here, here, d_send.at[0], d_recv.at[u], r, mate).start()
 
     def d_step(u):
         if u in DIRECT:
@@ -188,7 +190,7 @@
             arrived(u, 2)
         for m in far:
             here = slabs.at[u, slab(m)]
-            remote(here, here, d_send.at[u], d_recv.at[u], r, mate).start()
+            remote(here, here, d_send.at[0], d_recv.at[u], r, mate).start()
 
     stages = {"A": a_step, "B": b_step, "D": d_step}
     done = set()
@@ -212,13 +214,34 @@
         for item in PLAN.get(place, ()):
             step(item[0], int(item[1:]))
 
+    def drain():
+        direct = len(DIRECT)
+        plain = units - direct
+        sends = [
+            (slabs.at[:, pl.ds(0, zn), :, pl.ds(0, quarter)], z_send.at[0]),
+            (slabs.at[:, pl.ds(0, zn - 1), :, pl.ds(0, 2 * quarter)], a_send.at[0]),
+            (slabs.at[:, pl.ds(0, zn)], d_send.at[0]),
+            (stat_in.at[pl.ds(1, convs - 1), pl.ds(1, rows_n - 1)], t_send.at[1]),
+            (stat_in.at[0, pl.ds(1, rows_n - 1)], t_send.at[0]),
+        ]
+        if far:
+            sends += [
+                (slabs.at[pl.ds(0, direct), pl.ds(0, zn - 2), :, pl.ds(0, quarter)], a_send.at[1]),
+                (slabs.at[pl.ds(0, plain), pl.ds(0, zn - 2), :, pl.ds(0, quarter)], b_send.at[0]),
+            ]
+        for ref, send in sends:
+            remote(ref, ref, send, t_recv.at[0], r, mate).wait_send()
+        for down, up in ends:
+            pl.when(r < rows_n - 1)(lambda: down().wait_send())
+            pl.when(r > 0)(lambda: up().wait_send())
+
     def need(u):
         step("B" if u in DIRECT else "D", u)
 
     def assemble(u):
         arrived(u, 3)
         for d in range(batch_n):
-            wfull[u % taps, d * outs:(d + 1) * outs, :] = slabs[u, d, :, :depth]
+            wfull[order[u % taps], d * outs:(d + 1) * outs, :] = slabs[u, d, :, :depth]
 
     def assemble_zero(block):
         for d in range(batch_n):
@@ -255,23 +278,19 @@
 
         return down, up
 
-    sent = []
-
     def stat_start(s, total, square):
         stat_out[s] = jnp.concatenate([total, square, jnp.zeros((6, channels), jnp.float32)], axis=0)
         for j in range(1, rows_n):
-            copy = remote(stat_out.at[s], stat_in.at[s, j], t_send.at[s, j], t_recv.at[s, j],
-                          (r + j) % rows_n, b)
-            copy.start()
-            sent.append(copy)
+            remote(stat_out.at[s], stat_in.at[s, j], t_send.at[min(s, 1)], t_recv.at[s],
+                   (r + j) % rows_n, b).start()
 
     col = lax.broadcasted_iota(jnp.int32, (across, channels), 0)
 
     def normalize(s, ref):
         total = stat_out[s]
+        here = stat_in.at[s, pl.ds(1, rows_n - 1)]
+        remote(here, here, t_send.at[0], t_recv.at[s], r, mate).wait_recv()
         for j in range(1, rows_n):
-            here = stat_in.at[s, j]
-            remote(here, here, t_send.at[s, j], t_recv.at[s, j], r, mate).wait_recv()
             total = total + stat_in[s, j]
         high = total.astype(jnp.bfloat16).astype(jnp.float32)
         rest = total - high
@@ -287,7 +306,8 @@
 
         def put(at, v, valid):
             y = v.astype(jnp.float32) * scale + bias
-            a = y / (1.0 + jnp.exp(-y))
+            half = 0.5 * y
+            a = half + half * jnp.tanh(half)
             if valid is not None:
                 a = jnp.where(valid, a, 0.0)
             left = jnp.where(col == 0, 0.0, pltpu.roll(a, 1, 0))
@@ -328,42 +348,34 @@
                 jnp.sum(kept * kept, axis=0, keepdims=True))
 
     def convolve(s, source, put):
-        units_of = range(s * taps, (s + 1) * taps)
-        rows = cells - 2 * across
-        if s == 0:
-            edges(s, put)
-            for t, u in enumerate(units_of):
-                need(u)
-                assemble(u)
-                value = times(stk[t * across:t * across + cells, :], wfull[t])
-                if t < taps - 1:
-                    acc[...] = value if t == 0 else acc[...] + value
-                    if t == 0:
-                        plan("pre0")
-                    plan(f"tap{t}")
-            return keep(s, source, 0, acc[...] + value)
-        inner = None
-        for t, u in enumerate(units_of):
-            need(u)
-            assemble(u)
-            value = times(stk[(t + 1) * across:(t + 1) * across + rows, :], wfull[t])
-            inner = value if t == 0 else inner + value
-        middle = keep(s, source, across, inner)
-        plan(f"half{s}")
-        edges(s, put)
-        border = None
-        for t in range(taps):
-            low, high = t * across, (height - 1 + t) * across
-            both = jnp.concatenate([stk[low:low + across, :], stk[high:high + across, :]], axis=0)
-            value = times(both, wfull[t])
-            border = value if t == 0 else border + value
-        top = keep(s, source, 0, border[:across])
-        bottom = keep(s, source, cells - across, border[across:])
-        return middle[0] + top[0] + bottom[0], middle[1] + top[1] + bottom[1]
+        last = s % per_block == per_block - 1
+        total = None
+        for i in range(taps):
+            t = order[i]
+            if i == 0 or s == 0:
+                need(s * taps + i)
+                assemble(s * taps + i)
+            elif i == 1:
+                for j in range(1, taps):
+                    need(s * taps + j)
+                    assemble(s * taps + j)
+                if last:
+                    assemble_zero(s // per_block)
+                plan(f"edge{s}")
+            value = times(stk[t * across:t * across + cells, :], wfull[t])
+            if i == 0 or s == 0 and i < taps - 1:
+                acc[...] = value if i == 0 else acc[...] + value
+            else:
+                total = value if total is None else total + value
+            if i == 0:
+                plan(f"half{s}")
+                edges(s, put)
+            if s == 0:
+                plan(f"tap{i}")
+        return keep(s, source, 0, acc[...] + total)
 
     def zero_conv(s):
         block = s // per_block
-        assemble_zero(block)
         zeroed = times(fields[s], zfull[...])
         out_ref[block] = (skipv[block].astype(jnp.float32) + zeroed).astype(jnp.bfloat16)
 
@@ -409,20 +421,7 @@
             source = fields.at[s]
             zero_conv(s)
     need(units - 1)
-    for copy in sent:
-        copy.wait_send()
-    for u in range(units):
-        for stage, (ref, send, recv) in enumerate(totals(u)):
-            if stage != 2 or far and u not in DIRECT:
-                remote(ref, ref, send.at[u], recv.at[u], r, mate).wait_send()
-    for down, up in ends:
-        @pl.when(r < rows_n - 1)
-        def _():
-            down().wait_send()
-
-        @pl.when(r > 0)
-        def _():
-            up().wait_send()
+    drain()
 
 
 def on_device(rows_n, batch_n, control, unet_skips, norm_gains, norm_shifts, conv_weights, zero_weights):
@@ -461,12 +460,12 @@
             pltpu.VMEM((stages, 8, channels), jnp.float32),
             pltpu.VMEM((stages, rows_n, 8, channels), jnp.float32),
             dma((7,)),
-            dma((units,)), dma((units,)),
-            dma((units,)), dma((units,)),
-            dma((units,)), dma((units,)),
-            dma((units,)), dma((units,)),
+            dma((1,)), dma((units,)),
+            dma((2,)), dma((units,)),
+            dma((1,)), dma((units,)),
+            dma((1,)), dma((units,)),
             dma((stages, 2)), dma((stages, 2)),
-            dma((stages, rows_n)), dma((stages, rows_n)),
+            dma((2,)), dma((stages,)),
         ],
         compiler_params=pltpu.CompilerParams(
             collective_id=0, has_side_effects=True, vmem_limit_bytes=50 * 1024 * 1024),

time: 49.7 us -> 49.1 us (0.988)
  Pallas kernels: 48.6 us -> 48 us
    pallas_call x1, Pallas kernels: 48.6 us -> 48 us  [on_device(): pl.pallas_call(functools.partial(kernel, dims), out_shape=jax.ShapeDtypeS...]
where the time goes in v5:
time: 49.1 us; the launch traced here: 48.9 us
  Pallas kernels  48 us (98%)
  local copies, waits for them, and re-layouts  0.91 us (2%)
    pallas_call x1, Pallas kernels, on_device(): pl.pallas_call(functools.partial(kernel, dims), out_shape=jax.ShapeDtypeS...  48 us

profile of v5, /device:TPU:0, one launch (start us, length us, event | category | flops | bytes accessed | tf_op | source)
XLA Modules:
  0.0 48.9 jit_solution(786664574229919403)
XLA Ops:
  0.0 48.0 %shard_map.64 = bf16[2,576,320]{2,1,0:T(8,128)(2,1)S(1)} custom-call(bf16[576,320]{1,0:T(8,128)(2,1)} %bitcast.14, bf16[2,576,320]{2,1,0:T(8,128)(2,1)} %bitcast.13, f32[2,2,320]{2,1,0:T(2,128)} %gain_hbm.1, f32[2,2,320]{2,1,0:T(2,128)} %shift_hbm.1, bf16[12,40,960]{2,1,0:T(8,128)(2,1)} %bitcast.12, bf16[2,40,320]{2,1,0:T(8,128)(2,1)} %bitcast.15), custom_call_target="tpu_custom_call" | custom-call | tf_op jit(solution)/shard_map/pallas_call | solution.py:440
  48.0 0.9 %copy.9 = bf16[2,1,6,96,320]{4,3,2,1,0:T(8,128)(2,1)} copy(bf16[2,1,6,96,320]{4,3,2,1,0:T(8,128)(2,1)S(1)} %bitcast.11) | data formatting | bytes 1474560
